TPU v7x, 256 devices: a whole 4x4x8 slice. The times are simulated.
256 devices in a mesh: owner: 8 (over x, core), rows: 32 (over z, y).
Axes of the slice: x: 4, y: 4, z: 8, core: 2. Of those that a mesh axis runs over, the one named last changes fastest.
Arguments:
- w_down: float32 [16, 6400, 4096], P('owner', None, 'rows'), may hold values from -0.15625 to 0.15625
- avg_down: bfloat16 [16, 6400, 4096], P('owner', None, 'rows'), may hold values from -0.0390625 to 0.0390625
- router_weight: float32 [4096, 16], P('rows', 'owner'), may hold values from -0.09375 to 0.09375
- router_gain: float32 [4096], P('rows'), may hold values from 0.25 to 1.75
Outputs:
- serve_down: bfloat16 [16, 6400, 4096], P('owner', 'rows')
- scale_down: float32 [16, 6400], P('owner', 'rows')
- serve_router: bfloat16 [4096, 16], replicated
All inputs are finite; a program needn't handle non-finite values. Where the computation divides by a largest or mean magnitude, that divisor is 1e-20 or more.
Results may differ from a plain program's by a relative error of at most 0.001.
Values may be sent and summed in bfloat16 or wider, within the bound.
A program may use at most 64 MiB of HBM per device.

v0:
```python
import jax
import jax.numpy as jnp
from jax import lax
from jax.sharding import PartitionSpec as P

D_MODEL = 4096


def copy_for_each(x, axis):
    count = lax.axis_size(axis)
    return lax.all_to_all(jnp.broadcast_to(x[None], (count, *x.shape)), axis, 0, 0, tiled=True)


def over_copies(x, axis):
    everything = copy_for_each(x, axis)
    return jnp.sum(everything, axis=0)


def laid_out(parts, dim):
    shape = list(parts.shape[1:])
    shape[dim] *= parts.shape[0]
    return jnp.moveaxis(parts, 0, dim).reshape(shape)


def collect(x, axis, dim):
    return laid_out(copy_for_each(x, axis), dim)


def per_device(w_down, avg_down, router_weight, router_gain):
    fresh_down = w_down + avg_down.astype(jnp.float32)
    total_down = over_copies(jnp.sum(jnp.abs(fresh_down), axis=2), "rows")
    scale_down = total_down / D_MODEL
    narrow_down = (fresh_down / jnp.expand_dims(scale_down, 2)).astype(jnp.bfloat16)
    serve_down = lax.all_to_all(narrow_down, "rows", split_axis=1, concat_axis=2, tiled=True)
    scale_down = lax.dynamic_slice_in_dim(
        scale_down, lax.axis_index("rows") * serve_down.shape[1], serve_down.shape[1], axis=1
    )
    part_router = (router_weight * router_gain[:, None]).astype(jnp.bfloat16)
    row_router = collect(part_router, "rows", 0)
    serve_router = collect(row_router, "owner", 1)
    return (serve_down, scale_down, serve_router)


def solution(mesh):
    return jax.shard_map(
        per_device,
        mesh=mesh,
        in_specs=(
            P("owner", None, "rows"),
            P("owner", None, "rows"),
            P("rows", "owner"),
            P("rows"),
        ),
        out_specs=(P("owner", "rows", None), P("owner", "rows"), P()),
        check_vma=False,
    )
```

profile of v0, /device:TPU:1, one launch (start us, length us, event | category | flops | bytes accessed | tf_op | source)
XLA Modules:
  0.0 198.4 jit_solution(2779808520759683975)
XLA Ops:
  0.6 0.7 multiply_convert_fusion
  1.3 0.6 broadcast_in_dim.9
  1.9 12.0 %all-to-all-start.2 = ((bf16[32,128,2]{1,2,0:T(2,128)(2,1)}), bf16[32,128,2]{1,2,0:T(2,128)(2,1)S(1)}, u32[]{:S(2)}, u32[]{:S(2)}) async-start(bf16[32,128,2]{1,2,0:T(2,128)(2,1)} %broadcast_in_dim.9), calls=%async_computation.2 | async-start | bytes 32768 | tf_op jit(solution)/shard_map/all_to_all | solution.py:11
  14.0 5.6 %abs_reduce_fusion = f32[2,6400]{1,0:T(2,128)S(1)} fusion(f32[2,6400,128]{2,1,0:T(8,128)} %param.4, bf16[2,6400,128]{2,1,0:T(8,128)(2,1)} %param.5), kind=kLoop, calls=%fused_computation.1 | loop fusion | flops 6540800 | bytes 9881600 | tf_op jit(solution)/shard_map/reduce_sum | solution.py:31
  19.6 0.0 copy-start
  19.6 2.9 %all-to-all-done.2 = bf16[32,128,2]{1,2,0:T(2,128)(2,1)S(1)} async-done(((bf16[32,128,2]{1,2,0:T(2,128)(2,1)}), bf16[32,128,2]{1,2,0:T(2,128)(2,1)S(1)}, u32[]{:S(2)}, u32[]{:S(2)}) %all-to-all-start.2) | async-done | bytes 16416 | tf_op jit(solution)/shard_map/all_to_all | solution.py:11
  22.5 0.4 broadcast_in_dim.8
  22.9 46.1 %all_to_all.33 = f32[32,2,6400]{2,1,0:T(2,128)} all-to-all(f32[32,2,6400]{2,1,0:T(2,128)S(1)} %broadcast_in_dim.8), channel_id=1, replica_groups=mesh['owner'=8,'rows'=32] {'rows'}, dimensions={0} | all-to-all | bytes 3276800 | tf_op jit(solution)/shard_map/all_to_all | solution.py:11
  69.0 0.7 broadcast_in_dim.11
  69.7 6.9 %all-to-all-start.3 = ((bf16[8,4096,2]{1,2,0:T(2,128)(2,1)}), bf16[8,4096,2]{1,2,0:T(2,128)(2,1)S(1)}, u32[]{:S(2)}, u32[]{:S(2)}) async-start(bf16[8,4096,2]{1,2,0:T(2,128)(2,1)} %broadcast_in_dim.11), calls=%async_computation.3 | async-start | bytes 262144 | tf_op jit(solution)/shard_map/all_to_all | solution.py:11
  76.6 1.9 reduce_sum.19
  78.6 0.0 copy-done
  78.6 4.7 %divide_convert_fusion = bf16[2,6400,128]{2,1,0:T(8,128)(2,1)S(1)} fusion(f32[2,6400,128]{2,1,0:T(8,128)} %param.4, bf16[2,6400,128]{2,1,0:T(8,128)(2,1)S(1)} %copy-done, f32[2,6400]{1,0:T(2,128)S(1)} %broadcast_multiply_fusion), kind=kLoop, calls=%fused_computation | loop fusion | flops 6553600 | bytes 13158400 | tf_op jit(solution)/shard_map/convert_element_type | solution.py:33
  83.3 27.9 %copy.31 = bf16[2,6400,128]{2,0,1:T(2,128)(2,1)} copy(bf16[2,6400,128]{2,1,0:T(8,128)(2,1)S(1)} %divide_convert_fusion) | data formatting | bytes 6553600 | tf_op jit(solution)/shard_map/convert_element_type | solution.py:33
  111.2 0.0 all-to-all-done.3
  111.2 4.6 %all-to-all-start.1 = ((bf16[2,6400,128]{2,0,1:T(2,128)(2,1)}), bf16[2,6400,128]{2,0,1:T(2,128)(2,1)S(1)}, u32[]{:S(2)}, u32[]{:S(2)}) async-start(bf16[2,6400,128]{2,0,1:T(2,128)(2,1)} %copy.31), calls=%async_computation.1 | async-start | bytes 6553600 | tf_op jit(solution)/shard_map/all_to_all | solution.py:34
  115.8 0.7 reshape.16
  116.5 0.7 constant_dynamic-slice_fusion
  117.2 72.5 %all-to-all-done.1 = bf16[2,6400,128]{2,0,1:T(2,128)(2,1)S(1)} async-done(((bf16[2,6400,128]{2,0,1:T(2,128)(2,1)}), bf16[2,6400,128]{2,0,1:T(2,128)(2,1)S(1)}, u32[]{:S(2)}, u32[]{:S(2)}) %all-to-all-start.1) | async-done | bytes 3276832 | tf_op jit(solution)/shard_map/all_to_all | solution.py:34
  189.6 2.5 %copy.32 = bf16[2,200,32,128]{3,2,1,0:T(8,128)(2,1)} copy(bf16[2,200,32,128]{3,0,1,2:T(2,128)(2,1)S(1)} %bitcast.9) | data formatting | bytes 6553600 | tf_op jit(solution)/shard_map/all_to_all | solution.py:34
  192.2 6.2 %all_to_all.26 = bf16[2,200,4096]{2,1,0:T(8,128)(2,1)} reshape(bf16[2,200,32,128]{3,2,1,0:T(8,128)(2,1)} %copy.32) | data formatting | bytes 6553600 | tf_op jit(solution)/shard_map/all_to_all | solution.py:34
  (1 shorter events, 0.0 us)
Async XLA Ops:
  1.9 20.6 %all-to-all-start.2 = ((bf16[32,128,2]{1,2,0:T(2,128)(2,1)}), bf16[32,128,2]{1,2,0:T(2,128)(2,1)S(1)}, u32[]{:S(2)}, u32[]{:S(2)}) async-start(bf16[32,128,2]{1,2,0:T(2,128)(2,1)} %broadcast_in_dim.9), calls=%async_computation.2 | async-start | bytes 32768 | tf_op jit(solution)/shard_map/all_to_all | solution.py:11
  19.6 59.0 %copy-start = (bf16[2,6400,128]{2,1,0:T(8,128)(2,1)S(1)}, bf16[2,6400,128]{2,1,0:T(8,128)(2,1)}, u32[]{:S(2)}) copy-start(bf16[2,6400,128]{2,1,0:T(8,128)(2,1)} %param.5) | copy-start | bytes 9830404
  69.7 41.5 %all-to-all-start.3 = ((bf16[8,4096,2]{1,2,0:T(2,128)(2,1)}), bf16[8,4096,2]{1,2,0:T(2,128)(2,1)S(1)}, u32[]{:S(2)}, u32[]{:S(2)}) async-start(bf16[8,4096,2]{1,2,0:T(2,128)(2,1)} %broadcast_in_dim.11), calls=%async_computation.3 | async-start | bytes 262144 | tf_op jit(solution)/shard_map/all_to_all | solution.py:11
  111.2 78.4 %all-to-all-start.1 = ((bf16[2,6400,128]{2,0,1:T(2,128)(2,1)}), bf16[2,6400,128]{2,0,1:T(2,128)(2,1)S(1)}, u32[]{:S(2)}, u32[]{:S(2)}) async-start(bf16[2,6400,128]{2,0,1:T(2,128)(2,1)} %copy.31), calls=%async_computation.1 | async-start | bytes 6553600 | tf_op jit(solution)/shard_map/all_to_all | solution.py:34
where the time goes:
time: 202 us; the launch traced here: 198 us
  waiting for transfers between devices  75.4 us (37%)
  blocking collectives  46.1 us (23%)
  local copies, waits for them, and re-layouts  39.7 us (20%)
  starting transfers between devices  23.5 us (12%)
  other arithmetic  12.9 us (6%)
    all_to_all x1, waiting for transfers between devices, per_device(): lax.all_to_all(narrow_down, 'rows', split_axis=1, concat_axis=2, tiled=True)  72.5 us
    all_to_all x1, blocking collectives, copy_for_each(): lax.all_to_all(jnp.broadcast_to(x[None], (count, *x.shape)), axis, 0, 0,...  46.1 us
    convert_element_type x1, local copies, waits for them, and re-layouts, per_device(): (fresh_down / jnp.expand_dims(scale_down, 2)).astype(jnp.bfloat16)  27.9 us
    all_to_all x2, starting transfers between devices, copy_for_each(): lax.all_to_all(jnp.broadcast_to(x[None], (count, *x.shape)), axis, 0, 0,...  18.9 us
    all_to_all x2, local copies, waits for them, and re-layouts, per_device(): lax.all_to_all(narrow_down, 'rows', split_axis=1, concat_axis=2, tiled=True)  8.72 us
    reduce_sum x1, other arithmetic, per_device(): total_down = over_copies(jnp.sum(jnp.abs(fresh_down), axis=2), 'rows')  5.6 us
    convert_element_type x1, other arithmetic, per_device(): (fresh_down / jnp.expand_dims(scale_down, 2)).astype(jnp.bfloat16)  4.74 us
    all_to_all x1, starting transfers between devices, per_device(): lax.all_to_all(narrow_down, 'rows', split_axis=1, concat_axis=2, tiled=True)  4.61 us
  transfers between devices with their start and end apart: 3, of which 2 were waited for; matrix products, arithmetic and copies ran while one was open for 21% of the time, Pallas kernels for 0%

commit v1 on v0

v1 whole, which is shorter than its diff:
```python
import functools

import jax
import jax.numpy as jnp
from jax import lax
from jax.experimental import pallas as pl
from jax.experimental.pallas import tpu as pltpu
from jax.sharding import PartitionSpec as P

MESH = pl.DeviceIdType.MESH
LANES = 128
HEAD = 8
SPLIT = 96


def exchange(
    n_rows, n_owner, ny, d_model,
    w_ref, a_ref, rw_ref, rg_ref,
    out_ref, scale_ref, rall_ref,
    rwbuf, rgbuf, wbuf, abuf, stage, heads_out, heads_in, sums_out, sums_in, scales, mine, rpart, rrow,
    rw_sem, rg_sem, w_sem, a_sem, rs_send, rs_recv, ag_send, ag_recv, head_send, head_recv,
    bulk_send, bulk_recv, r1_send, r1_recv, r2_send, r2_recv,
):
    nz = n_rows // ny
    me = lax.axis_index("rows")
    own = lax.axis_index("owner")
    z, y = me // ny, lax.rem(me, ny)
    rows = out_ref.shape[1]
    groups = tuple((e, lo, hi) for e in range(2) for lo, hi in ((0, SPLIT), (SPLIT, rows)))
    body = pl.ds(2 * HEAD, rows - 2 * HEAD)

    def peer(d):
        return lax.rem(z + d // ny, nz) * ny + lax.rem(y + lax.rem(d, ny), ny)

    def lanes_of(r):
        return pl.ds(pl.multiple_of(r * LANES, LANES), LANES)

    def load(d):
        part = pl.ds(pl.multiple_of(peer(d) * rows, 8), rows)
        return (
            pltpu.make_async_copy(w_ref.at[:, part, :], wbuf.at[d], w_sem.at[d]),
            pltpu.make_async_copy(a_ref.at[:, part, :], abuf.at[d], a_sem.at[d]),
        )

    def remote(src, dst, send, recv, p):
        return pltpu.make_async_remote_copy(
            src_ref=src, dst_ref=dst, send_sem=send, recv_sem=recv,
            device_id={"rows": p}, device_id_type=MESH,
        )

    def rs(d, p, slot):
        return remote(sums_out.at[d], sums_in.at[slot], rs_send.at[d], rs_recv.at[slot], p)

    def ag(d, p, slot):
        return remote(mine, scales.at[slot], ag_send.at[d], ag_recv.at[slot], p)

    def head(h, d, p, slot):
        return remote(heads_out.at[h, d], heads_in.at[h, slot], head_send.at[h, d], head_recv.at[h, slot], p)

    def bulk(d, p, slot):
        return remote(stage.at[d], out_ref.at[:, body, lanes_of(slot)], bulk_send.at[d], bulk_recv.at[slot], p)

    def router_rows(d, p, slot):
        return remote(rpart, rrow.at[slot], r1_send.at[d], r1_recv.at[slot], p)

    def router_all(d, o, slot):
        return pltpu.make_async_remote_copy(
            src_ref=rrow, dst_ref=rall_ref.at[slot], send_sem=r2_send.at[d], recv_sem=r2_recv.at[slot],
            device_id={"owner": o}, device_id_type=MESH,
        )

    barrier = pltpu.get_barrier_semaphore()

    @pl.loop(1, n_rows)
    def _(d):
        pl.semaphore_signal(barrier, inc=1, device_id={"rows": peer(d)}, device_id_type=MESH)

    @pl.loop(1, n_owner)
    def _(d):
        pl.semaphore_signal(barrier, inc=1, device_id={"owner": lax.rem(own + d, n_owner)}, device_id_type=MESH)

    @pl.loop(0, n_rows)
    def _(d):
        for copy in load(d):
            copy.start()

    router = (
        pltpu.make_async_copy(rw_ref, rwbuf, rw_sem),
        pltpu.make_async_copy(rg_ref, rgbuf, rg_sem),
    )
    for copy in router:
        copy.start()
    for copy in router:
        copy.wait()
    part = (rwbuf[...] * rgbuf[...]).astype(jnp.bfloat16)
    rpart[...] = part
    rrow[me] = part
    eye = lax.broadcasted_iota(jnp.int32, (LANES, LANES), 0) == lax.broadcasted_iota(jnp.int32, (LANES, LANES), 1)

    def fresh(d, e, lo, hi):
        return wbuf[d, e, lo:hi, :] + abuf[d, e, lo:hi, :].astype(jnp.float32)

    def row_sums(x):
        size = jnp.abs(x)
        top = size.astype(jnp.bfloat16)
        low = (size - top.astype(jnp.float32)).astype(jnp.bfloat16)
        both = jnp.concatenate([top, low], axis=1)
        total = jnp.dot(both, jnp.ones((2 * LANES, LANES), jnp.bfloat16), preferred_element_type=jnp.float32)
        return jnp.sum(jnp.where(eye[: x.shape[0]], total, 0.0), axis=0, keepdims=True)

    def down_rows(v, count):
        spread = jnp.where(eye[:count], jnp.broadcast_to(v, (count, LANES)), 0.0)
        one = spread.astype(jnp.bfloat16)
        rest = spread - one.astype(jnp.float32)
        two = rest.astype(jnp.bfloat16)
        three = (rest - two.astype(jnp.float32)).astype(jnp.bfloat16)
        pieces = jnp.concatenate([one, two, three], axis=1)
        return jnp.dot(pieces, jnp.ones((3 * LANES, LANES), jnp.bfloat16), preferred_element_type=jnp.float32)

    @pl.loop(0, n_rows)
    def _(d):
        for copy in load(d):
            copy.wait()
        for g, (e, lo, hi) in enumerate(groups):
            x = fresh(d, e, lo, hi)
            if lo == 0:
                for h in range(2):
                    heads_out[h, d, e] = x[h * HEAD : (h + 1) * HEAD]
            sums_out[d, g : g + 1, :] = row_sums(x)

    pl.semaphore_wait(barrier, n_rows - 1 + n_owner - 1)

    @pl.loop(1, n_rows)
    def _(d):
        rs(d, peer(d), me).start()

    @pl.loop(1, n_rows)
    def _(d):
        head(0, d, peer(d), me).start()

    sums_in[me] = sums_out[0]
    heads_in[0, me] = heads_out[0, 0]
    heads_in[1, me] = heads_out[1, 0]

    @pl.loop(1, n_rows)
    def _(d):
        p = peer(d)
        rs(d, p, p).wait_recv()

    total = sums_in[0]
    for r in range(1, n_rows):
        total = total + sums_in[r]
    scale = total / d_model
    mine[...] = scale
    scale_ref[...] = scale
    scales[me] = scale

    @pl.loop(1, n_rows)
    def _(d):
        ag(d, peer(d), me).start()

    @pl.loop(1, n_rows)
    def _(d):
        head(1, d, peer(d), me).start()

    @pl.loop(1, n_rows)
    def _(d):
        router_rows(d, peer(d), me).start()

    def normalised(d, p, write):
        inverse = 1.0 / scales[p]
        for g, (e, lo, hi) in enumerate(groups):
            value = fresh(d, e, lo, hi) * down_rows(inverse[g : g + 1, :], hi - lo)
            first = 2 * HEAD if lo == 0 else 0
            write(e, lo + first, hi, value[first:].astype(jnp.bfloat16))

    def write_stage(d):
        def write(e, lo, hi, value):
            stage[d, e, lo - 2 * HEAD : hi - 2 * HEAD, :] = value
        return write

    def write_out(e, lo, hi, value):
        out_ref[e, lo:hi, lanes_of(me)] = value

    @pl.loop(1, n_rows)
    def _(d):
        p = peer(d)
        ag(d, p, p).wait_recv()
        normalised(d, p, write_stage(d))
        bulk(d, p, me).start()

    normalised(0, me, write_out)

    @pl.loop(1, n_rows)
    def _(d):
        p = peer(d)
        router_rows(d, p, p).wait_recv()

    @pl.loop(1, n_owner)
    def _(d):
        router_all(d, lax.rem(own + d, n_owner), own).start()

    rall_ref[own] = rrow[...]

    inverse = 1.0 / mine[...]
    factors = [down_rows(inverse[2 * e : 2 * e + 1, :], 2 * HEAD) for e in range(2)]

    @pl.loop(0, n_rows)
    def _(d):
        p = peer(d)

        @pl.when(d > 0)
        def _():
            head(0, d, p, p).wait_recv()
            head(1, d, p, p).wait_recv()

        for e in range(2):
            both = jnp.concatenate([heads_in[0, p, e], heads_in[1, p, e]], axis=0) * factors[e]
            out_ref[e, 0 : 2 * HEAD, lanes_of(p)] = both.astype(jnp.bfloat16)

    @pl.loop(1, n_rows)
    def _(d):
        p = peer(d)
        rs(d, p, me).wait_send()
        ag(d, p, me).wait_send()
        head(0, d, p, me).wait_send()
        head(1, d, p, me).wait_send()
        router_rows(d, p, me).wait_send()
        bulk(d, p, me).wait_send()
        bulk(d, p, p).wait_recv()

    @pl.loop(1, n_owner)
    def _(d):
        o = lax.rem(own + d, n_owner)
        router_all(d, o, own).wait_send()
        router_all(d, o, o).wait_recv()


def per_device(n_rows, n_owner, ny, d_model, w_down, avg_down, router_weight, router_gain):
    experts, all_rows, lanes = w_down.shape
    rows = all_rows // n_rows
    dma = pltpu.SemaphoreType.DMA
    f32, bf16 = jnp.float32, jnp.bfloat16
    serve, scale, router = pl.pallas_call(
        functools.partial(exchange, n_rows, n_owner, ny, d_model),
        out_shape=(
            pltpu.VMEM((experts, rows, n_rows * lanes), bf16),
            pltpu.VMEM((2 * experts, lanes), f32),
            pltpu.VMEM((n_owner, n_rows, 2, lanes), bf16),
        ),
        in_specs=[pl.BlockSpec(memory_space=pltpu.HBM)] * 4,
        out_specs=[pl.BlockSpec(memory_space=pltpu.VMEM)] * 3,
        scratch_shapes=[
            pltpu.VMEM((2, lanes), f32),
            pltpu.VMEM((1, lanes), f32),
            pltpu.VMEM((n_rows, experts, rows, lanes), f32),
            pltpu.VMEM((n_rows, experts, rows, lanes), bf16),
            pltpu.VMEM((n_rows, experts, rows - 2 * HEAD, lanes), bf16),
            pltpu.VMEM((2, n_rows, experts, HEAD, lanes), f32),
            pltpu.VMEM((2, n_rows, experts, HEAD, lanes), f32),
            pltpu.VMEM((n_rows, 2 * experts, lanes), f32),
            pltpu.VMEM((n_rows, 2 * experts, lanes), f32),
            pltpu.VMEM((n_rows, 2 * experts, lanes), f32),
            pltpu.VMEM((2 * experts, lanes), f32),
            pltpu.VMEM((2, lanes), bf16),
            pltpu.VMEM((n_rows, 2, lanes), bf16),
            dma, dma,
            dma((n_rows,)), dma((n_rows,)),
            dma((n_rows,)), dma((n_rows,)),
            dma((n_rows,)), dma((n_rows,)),
            dma((2, n_rows)), dma((2, n_rows)),
            dma((n_rows,)), dma((n_rows,)),
            dma((n_rows,)), dma((n_rows,)),
            dma((n_owner,)), dma((n_owner,)),
        ],
        compiler_params=pltpu.CompilerParams(
            collective_id=0, has_side_effects=True, vmem_limit_bytes=60 << 20
        ),
    )(w_down, avg_down, router_weight.T, router_gain[None, :])
    scale_down = jnp.concatenate(
        [scale.reshape(experts, 2, lanes)[:, 0, :SPLIT], scale.reshape(experts, 2, lanes)[:, 1, : rows - SPLIT]], axis=1
    )
    serve_router = jnp.transpose(router, (1, 3, 0, 2)).reshape(n_rows * lanes, 2 * n_owner)
    return serve, scale_down, serve_router


def solution(mesh):
    n_rows, n_owner = mesh.shape["rows"], mesh.shape["owner"]
    return jax.shard_map(
        functools.partial(per_device, n_rows, n_owner, 4, 4096),
        mesh=mesh,
        in_specs=(
            P("owner", None, "rows"),
            P("owner", None, "rows"),
            P("rows", "owner"),
            P("rows"),
        ),
        out_specs=(P("owner", "rows", None), P("owner", "rows"), P()),
        check_vma=False,
    )
```

time: 202 us -> 110 us (0.54); the launches traced: 198 us -> 109 us
  Pallas kernels: 0 us -> 106 us
  waiting for transfers between devices: 75.4 us -> 0 us
  blocking collectives: 46.1 us -> 0 us
  local copies, waits for them, and re-layouts: 39.7 us -> 2.44 us
  starting transfers between devices: 23.5 us -> 0 us
  other arithmetic: 12.9 us -> 0.65 us
    pallas_call x0 -> x1, Pallas kernels: none -> 106 us  [per_device(): pl.pallas_call(functools.partial(exchange, n_rows, n_owner, ny, d_model),...]
    all_to_all x3 -> x0, waiting for transfers between devices: 75.4 us -> none  [the longest x1 72.5 us: per_device(): lax.all_to_all(narrow_down, 'rows', split_axis=1, concat_axis=2, tiled=True)]
    all_to_all x1 -> x0, blocking collectives: 46.1 us -> none  [copy_for_each(): lax.all_to_all(jnp.broadcast_to(x[None], (count, *x.shape)), axis, 0, 0,...]
    convert_element_type x1 -> x0, local copies, waits for them, and re-layouts: 27.9 us -> none  [per_device(): (fresh_down / jnp.expand_dims(scale_down, 2)).astype(jnp.bfloat16)]
    all_to_all x3 -> x0, starting transfers between devices: 23.5 us -> none  [the longest x2 18.9 us: copy_for_each(): lax.all_to_all(jnp.broadcast_to(x[None], (count, *x.shape)), axis, 0, 0,...]
    all_to_all x2 -> x0, local copies, waits for them, and re-layouts: 8.72 us -> none  [per_device(): lax.all_to_all(narrow_down, 'rows', split_axis=1, concat_axis=2, tiled=True)]
    reduce_sum x2 -> x0, other arithmetic: 7.5 us -> none  [the longest x1 5.6 us: per_device(): total_down = over_copies(jnp.sum(jnp.abs(fresh_down), axis=2), 'rows')]
    convert_element_type x2 -> x0, other arithmetic: 5.43 us -> none  [the longest x1 4.74 us: per_device(): (fresh_down / jnp.expand_dims(scale_down, 2)).astype(jnp.bfloat16)]
  transfers between devices with their start and end apart: 3 -> 0, of which waited for: 2 -> 0; matrix products, arithmetic and copies ran while one was open for 21% -> 0% of each run, Pallas kernels for 0% -> 0%
where the time goes in v1:
time: 110 us; the launch traced here: 109 us
  Pallas kernels  106 us (96%)
  local copies, waits for them, and re-layouts  2.44 us (2%)
    pallas_call x1, Pallas kernels, per_device(): pl.pallas_call(functools.partial(exchange, n_rows, n_owner, ny, d_model),...  106 us
    unnamed x2, local copies, waits for them, and re-layouts  2.42 us

profile of v1, /device:TPU:1, one launch (start us, length us, event | category | flops | bytes accessed | tf_op | source)
XLA Modules:
  0.0 109.5 jit_solution(18275022648601884247)
XLA Ops:
  0.6 105.8 %shard_map.67 = (bf16[2,200,4096]{2,1,0:T(8,128)(2,1)S(1)}, f32[4,128]{1,0:T(4,128)S(1)}, bf16[8,32,2,128]{3,2,1,0:T(2,128)(2,1)S(1)}) custom-call(f32[2,6400,128]{2,1,0:T(8,128)} %w_ref.1, bf16[2,6400,128]{2,1,0:T(8,128)(2,1)} %a_ref.1, f32[2,128]{1,0:T(2,128)} %bitcast.24, f32[1,128]{1,0:T(1,128)} %bitcast.25), custom_call_target="tpu_custom_call" | custom-call | tf_op jit(solution)/shard_map/pallas_call | solution.py:244
  106.4 1.7 %copy.18 = bf16[2,200,4096]{2,1,0:T(8,128)(2,1)} copy(bf16[2,200,4096]{2,1,0:T(8,128)(2,1)S(1)} %get-tuple-element.9) | data formatting | bytes 6553600
  108.1 0.7 pad_maximum_fusion
  108.8 0.7 copy.16
  (3 shorter events, 0.0 us)

commit v2 on v0

v2 whole, which is shorter than its diff:
```python
import functools

import jax
import jax.numpy as jnp
from jax import lax
from jax.experimental import pallas as pl
from jax.experimental.pallas import tpu as pltpu
from jax.sharding import PartitionSpec as P

MESH = pl.DeviceIdType.MESH
LANES = 128
UNIT = 8
HEADS = (1, 1)
HEAD = UNIT * sum(HEADS)
SPLIT = 128
FAR = (4, 3, 5, 2, 6, 1, 7, 0)
NEAR = (0, 1, 5, 2, 4, 6, 3, 7)


def exchange(
    n_rows, n_owner, ny, d_model,
    w_ref, a_ref, rw_ref, rg_ref,
    out_ref, scale_ref, router_ref,
    rwbuf, rgbuf, wbuf, abuf, stage, ho_0, ho_1, hi_0, hi_1, sums_out, sums_in, scales, mine,
    rpart, rrow, rall, rtile,
    rw_sem, rg_sem, own_sem, w_sem, a_sem, rs_send, rs_recv, ag_send, ag_recv, head_send, head_recv,
    bulk_send, bulk_recv, r1_send, r1_recv, r2_send, r2_recv,
):
    nz = n_rows // ny
    me = lax.axis_index("rows")
    own = lax.axis_index("owner")
    z, y = me // ny, lax.rem(me, ny)
    experts, rows = out_ref.shape[:2]
    groups = tuple((e, lo, hi) for e in range(experts) for lo, hi in ((0, SPLIT), (SPLIT, rows)))
    body = pl.ds(HEAD, rows - HEAD)
    heads_out, heads_in = (ho_0, ho_1), (hi_0, hi_1)
    others = pl.ds(0, n_rows - 1)

    def pick(table, i):
        if isinstance(i, int):
            return table[i]
        value = jnp.int32(table[0])
        for k in range(1, len(table)):
            value = jnp.where(i == k, table[k], value)
        return value

    def plane(i):
        return lax.rem(z + pick(NEAR, i), nz)

    def peers(table):
        return [
            lax.rem(z + dz, nz) * ny + lax.rem(y + dy, ny)
            for dz in table for dy in (2, 1, 3, 0) if (dz, dy) != (0, 0)
        ]

    def owners():
        return [lax.rem(own + d, n_owner) for d in range(1, n_owner)]

    def lanes_of(r):
        return pl.ds(pl.multiple_of(r * LANES, LANES), LANES)

    def load(i):
        part = pl.ds(plane(i) * ny, ny)
        return (
            pltpu.make_async_copy(w_ref.at[:, part], wbuf.at[i], w_sem.at[i]),
            pltpu.make_async_copy(a_ref.at[:, part], abuf.at[i], a_sem.at[i]),
        )

    def remote(src, dst, send, recv, p):
        return pltpu.make_async_remote_copy(
            src_ref=src, dst_ref=dst, send_sem=send, recv_sem=recv,
            device_id={"rows": p}, device_id_type=MESH,
        )

    def router_all(src, dst, o):
        return pltpu.make_async_remote_copy(
            src_ref=src, dst_ref=dst, send_sem=r2_send, recv_sem=r2_recv,
            device_id={"owner": o}, device_id_type=MESH,
        )

    def own_block():
        return pltpu.make_async_copy(stage.at[y], out_ref.at[:, body, lanes_of(me)], own_sem)

    far = peers(FAR)
    next_one = far[0]
    barrier = pltpu.get_barrier_semaphore()
    for p in far:
        pl.semaphore_signal(barrier, inc=1, device_id={"rows": p}, device_id_type=MESH)
    for o in owners():
        pl.semaphore_signal(barrier, inc=1, device_id={"owner": o}, device_id_type=MESH)

    for i in range(nz):
        for copy in load(i):
            copy.start()
    router = (
        pltpu.make_async_copy(rw_ref, rwbuf, rw_sem),
        pltpu.make_async_copy(rg_ref, rgbuf, rg_sem),
    )
    for copy in router:
        copy.start()

    eye = lax.broadcasted_iota(jnp.int32, (LANES, LANES), 0) == lax.broadcasted_iota(jnp.int32, (LANES, LANES), 1)

    def fresh(i, e, k, lo, hi):
        return wbuf[i, e, k, lo:hi, :] + abuf[i, e, k, lo:hi, :].astype(jnp.float32)

    def row_sums(x):
        size = jnp.abs(x)
        top = size.astype(jnp.bfloat16)
        low = (size - top.astype(jnp.float32)).astype(jnp.bfloat16)
        both = jnp.concatenate([top, low], axis=1)
        total = jnp.dot(both, jnp.ones((2 * LANES, LANES), jnp.bfloat16), preferred_element_type=jnp.float32)
        return jnp.sum(jnp.where(eye[: x.shape[0]], total, 0.0), axis=0, keepdims=True)

    def down_rows(v, count):
        spread = jnp.where(eye[:count], jnp.broadcast_to(v, (count, LANES)), 0.0)
        one = spread.astype(jnp.bfloat16)
        rest = spread - one.astype(jnp.float32)
        two = rest.astype(jnp.bfloat16)
        three = (rest - two.astype(jnp.float32)).astype(jnp.bfloat16)
        pieces = jnp.concatenate([one, two, three], axis=1)
        return jnp.dot(pieces, jnp.ones((3 * LANES, LANES), jnp.bfloat16), preferred_element_type=jnp.float32)

    @pl.loop(0, nz)
    def _(i):
        for copy in load(i):
            copy.wait()
        base = plane(i) * ny
        for k in range(ny):
            for g, (e, lo, hi) in enumerate(groups):
                x = fresh(i, e, k, lo, hi)
                if lo == 0:
                    first = 0
                    for h, count in enumerate(HEADS):
                        heads_out[h][base + k, e] = x[first : first + count * UNIT]
                        first += count * UNIT
                sums_out[base + k, g : g + 1, :] = row_sums(x)

    for copy in router:
        copy.wait()
    part = (rwbuf[...] * rgbuf[...]).astype(jnp.bfloat16)
    rpart[...] = part
    rrow[me] = part

    pl.semaphore_wait(barrier, n_rows - 1 + n_owner - 1)

    for p in far:
        remote(sums_out.at[p], sums_in.at[me], rs_send, rs_recv, p).start()
    for p in far:
        remote(heads_out[0].at[p], heads_in[0].at[me], head_send.at[0], head_recv.at[0], p).start()

    sums_in[me] = sums_out[me]
    for h in range(len(HEADS)):
        heads_in[h][me] = heads_out[h][me]

    remote(sums_out.at[others], sums_in.at[others], rs_send, rs_recv, next_one).wait_recv()

    total = sums_in[0]
    for r in range(1, n_rows):
        total = total + sums_in[r]
    scale = total / d_model
    mine[...] = scale
    scales[me] = scale

    for p in far:
        remote(mine, scales.at[me], ag_send, ag_recv.at[z], p).start()
    for h in range(1, len(HEADS)):
        for p in far:
            remote(heads_out[h].at[p], heads_in[h].at[me], head_send.at[h], head_recv.at[h], p).start()
    for p in far:
        remote(rpart, rrow.at[me], r1_send, r1_recv, p).start()

    for g, (e, lo, hi) in enumerate(groups):
        scale_ref[e : e + 1, lo:hi] = scale[g : g + 1, : hi - lo]

    def normalise(i, k, p):
        inverse = 1.0 / scales[p]
        for g, (e, lo, hi) in enumerate(groups):
            value = fresh(i, e, k, lo, hi) * down_rows(inverse[g : g + 1, :], hi - lo)
            first = HEAD if lo == 0 else 0
            stage[i * ny + k, e, lo + first - HEAD : hi - HEAD, :] = value[first:].astype(jnp.bfloat16)

    def wait_scales(i, count):
        got = scales.at[pl.ds(0, count)]
        remote(got, got, ag_send, ag_recv.at[plane(i)], next_one).wait_recv()

    def send(i, k, p):
        remote(stage.at[i * ny + k], out_ref.at[:, body, lanes_of(me)], bulk_send, bulk_recv, p).start()

    turns = [lax.rem(y + k, ny) for k in range(ny)]

    @pl.loop(1, nz)
    def _(i):
        base = plane(i) * ny
        wait_scales(i, ny)
        for k in turns:
            normalise(i, k, base + k)
        for k in turns:
            send(i, k, base + k)

    wait_scales(0, ny - 1)
    for k in turns:
        normalise(0, k, z * ny + k)
    own_block().start()
    for k in turns[1:]:
        send(0, k, z * ny + k)

    remote(rrow.at[others], rrow.at[others], r1_send, r1_recv, next_one).wait_recv()
    for o in owners():
        router_all(rrow, rall.at[own], o).start()
    rall[own] = rrow[...]

    inverse = 1.0 / mine[...]
    factors = [down_rows(inverse[2 * e : 2 * e + 1, :], HEAD) for e in range(experts)]
    for h in range(len(HEADS)):
        got = heads_in[h].at[others]
        remote(got, got, head_send.at[h], head_recv.at[h], next_one).wait_recv()

    @pl.loop(0, n_rows // ny)
    def _(i):
        for k in range(ny):
            r = i * ny + k
            for e in range(experts):
                whole = jnp.concatenate([heads_in[h][r, e] for h in range(len(HEADS))], axis=0) * factors[e]
                out_ref[e, 0:HEAD, lanes_of(r)] = whole.astype(jnp.bfloat16)

    got = rall.at[pl.ds(0, n_owner - 1)]
    router_all(got, got, owners()[0]).wait()

    @pl.loop(0, n_rows)
    def _(r):
        for o in range(n_owner):
            rtile[2 * o : 2 * o + 2, :] = rall[o, r].astype(jnp.float32)
        router_ref[:, lanes_of(r)] = rtile[...].astype(jnp.bfloat16)

    own_block().wait()
    remote(sums_out.at[others], sums_in.at[others], rs_send, rs_recv, next_one).wait_send()
    remote(scales.at[others], scales.at[others], ag_send, rs_recv, next_one).wait_send()
    for h in range(len(HEADS)):
        got = heads_in[h].at[others]
        remote(got, got, head_send.at[h], head_recv.at[h], next_one).wait_send()
    remote(rrow.at[others], rrow.at[others], r1_send, r1_recv, next_one).wait_send()
    landed = out_ref.at[:, body, pl.ds(0, (n_rows - 1) * LANES)]
    remote(stage.at[others], landed, bulk_send, bulk_recv, next_one).wait()


def hand_over(serve_ref, scale_ref, router_ref, serve_out, scale_out, router_out, serve_sem, scale_sem, router_sem):
    pieces = serve_sem.shape[0]
    rows = serve_ref.shape[1] * serve_ref.shape[0] // pieces
    per = pieces // serve_ref.shape[0]
    copies = [
        pltpu.make_async_copy(
            serve_ref.at[i // per, pl.ds(i % per * rows, rows), :],
            serve_out.at[i // per, pl.ds(i % per * rows, rows), :],
            serve_sem.at[i],
        )
        for i in range(pieces)
    ]
    copies.append(pltpu.make_async_copy(scale_ref, scale_out, scale_sem))
    copies.append(pltpu.make_async_copy(router_ref, router_out, router_sem))
    for copy in copies:
        copy.start()
    for copy in copies:
        copy.wait()


def per_device(n_rows, n_owner, ny, d_model, w_down, avg_down, router_weight, router_gain):
    experts, all_rows, lanes = w_down.shape
    rows = all_rows // n_rows
    dma = pltpu.SemaphoreType.DMA

    def split(x):
        return x.reshape(experts, n_rows, rows, lanes)

    f32, bf16 = jnp.float32, jnp.bfloat16
    shapes = (
        ((experts, rows, n_rows * lanes), bf16),
        ((experts, rows), f32),
        ((2 * n_owner, n_rows * lanes), bf16),
    )
    serve, scale, router = pl.pallas_call(
        functools.partial(exchange, n_rows, n_owner, ny, d_model),
        out_shape=tuple(pltpu.VMEM(shape, dtype) for shape, dtype in shapes),
        in_specs=[pl.BlockSpec(memory_space=pltpu.HBM)] * 4,
        out_specs=[pl.BlockSpec(memory_space=pltpu.VMEM)] * 3,
        scratch_shapes=[
            pltpu.VMEM((2, lanes), f32),
            pltpu.VMEM((1, lanes), f32),
            pltpu.VMEM((n_rows // ny, experts, ny, rows, lanes), f32),
            pltpu.VMEM((n_rows // ny, experts, ny, rows, lanes), bf16),
            pltpu.VMEM((n_rows, experts, rows - HEAD, lanes), bf16),
            *[pltpu.VMEM((n_rows, experts, UNIT * count, lanes), f32) for count in HEADS],
            *[pltpu.VMEM((n_rows, experts, UNIT * count, lanes), f32) for count in HEADS],
            pltpu.VMEM((n_rows, 2 * experts, lanes), f32),
            pltpu.VMEM((n_rows, 2 * experts, lanes), f32),
            pltpu.VMEM((n_rows, 2 * experts, lanes), f32),
            pltpu.VMEM((2 * experts, lanes), f32),
            pltpu.VMEM((2, lanes), bf16),
            pltpu.VMEM((n_rows, 2, lanes), bf16),
            pltpu.VMEM((n_owner, n_rows, 2, lanes), bf16),
            pltpu.VMEM((2 * n_owner, lanes), f32),
            dma, dma, dma,
            dma((n_rows // ny,)), dma((n_rows // ny,)),
            dma, dma,
            dma, dma((n_rows // ny,)),
            dma((len(HEADS),)), dma((len(HEADS),)),
            dma, dma,
            dma, dma,
            dma, dma,
        ],
        compiler_params=pltpu.CompilerParams(
            collective_id=0, has_side_effects=True, vmem_limit_bytes=60 << 20
        ),
    )(split(w_down), split(avg_down), router_weight.T, router_gain[None, :])
    serve, scale, router = pl.pallas_call(
        hand_over,
        out_shape=tuple(jax.ShapeDtypeStruct(shape, dtype) for shape, dtype in shapes),
        in_specs=[pl.BlockSpec(memory_space=pltpu.VMEM)] * 3,
        out_specs=[pl.BlockSpec(memory_space=pl.ANY)] * 3,
        scratch_shapes=[dma((2 * experts if rows % 16 == 0 else experts * 5,)), dma, dma],
        compiler_params=pltpu.CompilerParams(vmem_limit_bytes=4 << 20),
    )(serve, scale, router)
    return serve, scale, router.T


def solution(mesh):
    n_rows, n_owner = mesh.shape["rows"], mesh.shape["owner"]
    return jax.shard_map(
        functools.partial(per_device, n_rows, n_owner, 4, 4096),
        mesh=mesh,
        in_specs=(
            P("owner", None, "rows"),
            P("owner", None, "rows"),
            P("rows", "owner"),
            P("rows"),
        ),
        out_specs=(P("owner", "rows", None), P("owner", "rows"), P()),
        check_vma=False,
    )
```

time: 202 us -> 96.3 us (0.48); the launches traced: 198 us -> 96.2 us
  Pallas kernels: 0 us -> 95.6 us
  waiting for transfers between devices: 75.4 us -> 0 us
  blocking collectives: 46.1 us -> 0 us
  local copies, waits for them, and re-layouts: 39.7 us -> 0 us
  starting transfers between devices: 23.5 us -> 0 us
  other arithmetic: 12.9 us -> 0 us
    pallas_call x0 -> x2, Pallas kernels: none -> 95.6 us  [the longest x1 93.8 us: per_device(): pl.pallas_call(functools.partial(exchange, n_rows, n_owner, ny, d_model),...]
    all_to_all x3 -> x0, waiting for transfers between devices: 75.4 us -> none  [the longest x1 72.5 us: per_device(): lax.all_to_all(narrow_down, 'rows', split_axis=1, concat_axis=2, tiled=True)]
    all_to_all x1 -> x0, blocking collectives: 46.1 us -> none  [copy_for_each(): lax.all_to_all(jnp.broadcast_to(x[None], (count, *x.shape)), axis, 0, 0,...]
    convert_element_type x1 -> x0, local copies, waits for them, and re-layouts: 27.9 us -> none  [per_device(): (fresh_down / jnp.expand_dims(scale_down, 2)).astype(jnp.bfloat16)]
    all_to_all x3 -> x0, starting transfers between devices: 23.5 us -> none  [the longest x2 18.9 us: copy_for_each(): lax.all_to_all(jnp.broadcast_to(x[None], (count, *x.shape)), axis, 0, 0,...]
    all_to_all x2 -> x0, local copies, waits for them, and re-layouts: 8.72 us -> none  [per_device(): lax.all_to_all(narrow_down, 'rows', split_axis=1, concat_axis=2, tiled=True)]
    reduce_sum x2 -> x0, other arithmetic: 7.5 us -> none  [the longest x1 5.6 us: per_device(): total_down = over_copies(jnp.sum(jnp.abs(fresh_down), axis=2), 'rows')]
    convert_element_type x2 -> x0, other arithmetic: 5.43 us -> none  [the longest x1 4.74 us: per_device(): (fresh_down / jnp.expand_dims(scale_down, 2)).astype(jnp.bfloat16)]
  transfers between devices with their start and end apart: 3 -> 0, of which waited for: 2 -> 0; matrix products, arithmetic and copies ran while one was open for 21% -> 0% of each run, Pallas kernels for 0% -> 0%
where the time goes in v2:
time: 96.3 us; the launch traced here: 96.2 us
  Pallas kernels  95.6 us (99%)
    pallas_call x1, Pallas kernels, per_device(): pl.pallas_call(functools.partial(exchange, n_rows, n_owner, ny, d_model),...  93.8 us

profile of v2, /device:TPU:1, one launch (start us, length us, event | category | flops | bytes accessed | tf_op | source)
XLA Modules:
  0.0 96.2 jit_solution(12705157738663603997)
XLA Ops:
  0.6 93.8 %shard_map.67 = (bf16[2,200,4096]{2,1,0:T(8,128)(2,1)S(1)}, f32[2,200]{1,0:T(2,128)S(1)}, bf16[16,4096]{1,0:T(8,128)(2,1)S(1)}) custom-call(f32[2,32,200,128]{3,2,1,0:T(8,128)} %bitcast.5, bf16[2,32,200,128]{3,2,1,0:T(8,128)(2,1)} %bitcast.6, f32[2,128]{1,0:T(2,128)} %bitcast.7, f32[1,128]{1,0:T(1,128)} %bitcast.8), custom_call_target="tpu_custom_call" | custom-call | tf_op jit(solution)/shard_map/pallas_call | solution.py:281
  94.4 1.8 %shard_map.68 = (bf16[2,200,4096]{2,1,0:T(8,128)(2,1)}, f32[2,200]{1,0:T(2,128)}, bf16[16,4096]{1,0:T(8,128)(2,1)}) custom-call(bf16[2,200,4096]{2,1,0:T(8,128)(2,1)S(1)} %get-tuple-element.9.serve_ref, f32[2,200]{1,0:T(2,128)S(1)} %get-tuple-element.10.scale_ref, bf16[16,4096]{1,0:T(8,128)(2,1)S(1)} %get-tuple-element.11.router_ref), custom_call_target="tpu_custom_call" | custom-call | tf_op jit(solution)/shard_map/pallas_call | solution.py:315

commit v3 on v2

--- a/solution.py
+++ b/solution.py
@@ -1,4 +1,5 @@
 import functools
+import math
 
 import jax
 import jax.numpy as jnp
@@ -9,9 +10,11 @@
 
 MESH = pl.DeviceIdType.MESH
 LANES = 128
-UNIT = 8
-HEADS = (1, 1)
-HEAD = UNIT * sum(HEADS)
+HEADS = (16, 16)
+HEAD = sum(HEADS)
+TINY = 1e-30
+SPAN = 250.0
+LOW = -125.0
 SPLIT = 128
 FAR = (4, 3, 5, 2, 6, 1, 7, 0)
 NEAR = (0, 1, 5, 2, 4, 6, 3, 7)
@@ -101,6 +104,19 @@
 
     eye = lax.broadcasted_iota(jnp.int32, (LANES, LANES), 0) == lax.broadcasted_iota(jnp.int32, (LANES, LANES), 1)
 
+    beside = lax.broadcasted_iota(jnp.int32, (HEAD, LANES), 1) == lax.broadcasted_iota(jnp.int32, (HEAD, LANES), 0) + (rows - SPLIT)
+
+    def encode(x):
+        size = jnp.abs(x)
+        most = jnp.maximum(jnp.max(size, axis=1, keepdims=True), TINY)
+        code = jnp.exp2(size * (SPAN / most) + LOW)
+        return jnp.where(x < 0, -code, code).astype(jnp.bfloat16), most
+
+    def decode(code, most):
+        code = code.astype(jnp.float32)
+        size = (jnp.log(jnp.abs(code)) * (1.0 / math.log(2.0)) - LOW) * (most / SPAN)
+        return jnp.where(code < 0, -size, size)
+
     def fresh(i, e, k, lo, hi):
         return wbuf[i, e, k, lo:hi, :] + abuf[i, e, k, lo:hi, :].astype(jnp.float32)
 
@@ -129,12 +145,16 @@
         for k in range(ny):
             for g, (e, lo, hi) in enumerate(groups):
                 x = fresh(i, e, k, lo, hi)
+                total = row_sums(x)
                 if lo == 0:
+                    code, most = encode(x[:HEAD])
                     first = 0
                     for h, count in enumerate(HEADS):
-                        heads_out[h][base + k, e] = x[first : first + count * UNIT]
-                        first += count * UNIT
-                sums_out[base + k, g : g + 1, :] = row_sums(x)
+                        heads_out[h][base + k, e] = code[first : first + count]
+                        first += count
+                else:
+                    total = total + jnp.sum(jnp.where(beside, most, 0.0), axis=0, keepdims=True)
+                sums_out[base + k, g : g + 1, :] = total
 
     for copy in router:
         copy.wait()
@@ -221,8 +241,10 @@
         for k in range(ny):
             r = i * ny + k
             for e in range(experts):
-                whole = jnp.concatenate([heads_in[h][r, e] for h in range(len(HEADS))], axis=0) * factors[e]
-                out_ref[e, 0:HEAD, lanes_of(r)] = whole.astype(jnp.bfloat16)
+                code = jnp.concatenate([heads_in[h][r, e] for h in range(len(HEADS))], axis=0)
+                row = jnp.broadcast_to(sums_in[r, 2 * e + 1 : 2 * e + 2, :], (HEAD, LANES))
+                most = jnp.sum(jnp.where(beside, row, 0.0), axis=1, keepdims=True)
+                out_ref[e, 0:HEAD, lanes_of(r)] = (decode(code, most) * factors[e]).astype(jnp.bfloat16)
 
     got = rall.at[pl.ds(0, n_owner - 1)]
     router_all(got, got, owners()[0]).wait()
@@ -289,8 +311,8 @@
             pltpu.VMEM((n_rows // ny, experts, ny, rows, lanes), f32),
             pltpu.VMEM((n_rows // ny, experts, ny, rows, lanes), bf16),
             pltpu.VMEM((n_rows, experts, rows - HEAD, lanes), bf16),
-            *[pltpu.VMEM((n_rows, experts, UNIT * count, lanes), f32) for count in HEADS],
-            *[pltpu.VMEM((n_rows, experts, UNIT * count, lanes), f32) for count in HEADS],
+            *[pltpu.VMEM((n_rows, experts, count, lanes), bf16) for count in HEADS],
+            *[pltpu.VMEM((n_rows, experts, count, lanes), bf16) for count in HEADS],
             pltpu.VMEM((n_rows, 2 * experts, lanes), f32),
             pltpu.VMEM((n_rows, 2 * experts, lanes), f32),
             pltpu.VMEM((n_rows, 2 * experts, lanes), f32),

time: 96.3 us -> 90.7 us (0.942)
  Pallas kernels: 95.6 us -> 89.9 us
    pallas_call x1, Pallas kernels: 93.8 us -> 88.1 us  [per_device(): pl.pallas_call(functools.partial(exchange, n_rows, n_owner, ny, d_model),...]
where the time goes in v3:
time: 90.7 us; the launch traced here: 90.6 us
  Pallas kernels  89.9 us (99%)
    pallas_call x1, Pallas kernels, per_device(): pl.pallas_call(functools.partial(exchange, n_rows, n_owner, ny, d_model),...  88.1 us
    pallas_call x1, Pallas kernels, per_device(): pl.pallas_call(hand_over, out_shape=tuple((jax.ShapeDtypeStruct(shape, dt...  1.84 us

profile of v3, /device:TPU:1, one launch (start us, length us, event | category | flops | bytes accessed | tf_op | source)
XLA Modules:
  0.0 90.6 jit_solution(11481569100263801298)
XLA Ops:
  0.6 88.1 %shard_map.67 = (bf16[2,200,4096]{2,1,0:T(8,128)(2,1)S(1)}, f32[2,200]{1,0:T(2,128)S(1)}, bf16[16,4096]{1,0:T(8,128)(2,1)S(1)}) custom-call(f32[2,32,200,128]{3,2,1,0:T(8,128)} %bitcast.5, bf16[2,32,200,128]{3,2,1,0:T(8,128)(2,1)} %bitcast.6, f32[2,128]{1,0:T(2,128)} %bitcast.7, f32[1,128]{1,0:T(1,128)} %bitcast.8), custom_call_target="tpu_custom_call" | custom-call | tf_op jit(solution)/shard_map/pallas_call | solution.py:303
  88.7 1.8 %shard_map.68 = (bf16[2,200,4096]{2,1,0:T(8,128)(2,1)}, f32[2,200]{1,0:T(2,128)}, bf16[16,4096]{1,0:T(8,128)(2,1)}) custom-call(bf16[2,200,4096]{2,1,0:T(8,128)(2,1)S(1)} %get-tuple-element.9.serve_ref, f32[2,200]{1,0:T(2,128)S(1)} %get-tuple-element.10.scale_ref, bf16[16,4096]{1,0:T(8,128)(2,1)S(1)} %get-tuple-element.11.router_ref), custom_call_target="tpu_custom_call" | custom-call | tf_op jit(solution)/shard_map/pallas_call | solution.py:337

commit v4 on v3

--- a/solution.py
+++ b/solution.py
@@ -10,7 +10,7 @@
 
 MESH = pl.DeviceIdType.MESH
 LANES = 128
-HEADS = (16, 16)
+HEADS = (16, 8, 16)
 HEAD = sum(HEADS)
 TINY = 1e-30
 SPAN = 250.0
@@ -24,7 +24,7 @@
     n_rows, n_owner, ny, d_model,
     w_ref, a_ref, rw_ref, rg_ref,
     out_ref, scale_ref, router_ref,
-    rwbuf, rgbuf, wbuf, abuf, stage, ho_0, ho_1, hi_0, hi_1, sums_out, sums_in, scales, mine,
+    rwbuf, rgbuf, wbuf, abuf, stage, ho_0, ho_1, ho_2, hi_0, hi_1, hi_2, sums_out, sums_in, scales, mine,
     rpart, rrow, rall, rtile,
     rw_sem, rg_sem, own_sem, w_sem, a_sem, rs_send, rs_recv, ag_send, ag_recv, head_send, head_recv,
     bulk_send, bulk_recv, r1_send, r1_recv, r2_send, r2_recv,
@@ -36,7 +36,7 @@
     experts, rows = out_ref.shape[:2]
     groups = tuple((e, lo, hi) for e in range(experts) for lo, hi in ((0, SPLIT), (SPLIT, rows)))
     body = pl.ds(HEAD, rows - HEAD)
-    heads_out, heads_in = (ho_0, ho_1), (hi_0, hi_1)
+    heads_out, heads_in = (ho_0, ho_1, ho_2), (hi_0, hi_1, hi_2)
     others = pl.ds(0, n_rows - 1)
 
     def pick(table, i):
@@ -62,12 +62,12 @@
     def lanes_of(r):
         return pl.ds(pl.multiple_of(r * LANES, LANES), LANES)
 
-    def load(i):
-        part = pl.ds(plane(i) * ny, ny)
-        return (
-            pltpu.make_async_copy(w_ref.at[:, part], wbuf.at[i], w_sem.at[i]),
-            pltpu.make_async_copy(a_ref.at[:, part], abuf.at[i], a_sem.at[i]),
-        )
+    def load(i, whole=True):
+        part, cut = pl.ds(plane(i) * ny, ny), body if whole else pl.ds(0, HEAD)
+        return [
+            pltpu.make_async_copy(ref.at[:, part, cut], buf.at[i, :, :, cut], sem.at[int(whole), i])
+            for ref, buf, sem in ((w_ref, wbuf, w_sem), (a_ref, abuf, a_sem))
+        ]
 
     def remote(src, dst, send, recv, p):
         return pltpu.make_async_remote_copy(
@@ -92,9 +92,10 @@
     for o in owners():
         pl.semaphore_signal(barrier, inc=1, device_id={"owner": o}, device_id_type=MESH)
 
-    for i in range(nz):
-        for copy in load(i):
-            copy.start()
+    for whole in (False, True):
+        for i in range(nz):
+            for copy in load(i, whole):
+                copy.start()
     router = (
         pltpu.make_async_copy(rw_ref, rwbuf, rw_sem),
         pltpu.make_async_copy(rg_ref, rgbuf, rg_sem),
@@ -139,22 +140,34 @@
 
     @pl.loop(0, nz)
     def _(i):
+        for copy in load(i, False):
+            copy.wait()
+        base = plane(i) * ny
+        for k in range(ny):
+            for e in range(experts):
+                code, most = encode(fresh(i, e, k, 0, HEAD))
+                first = 0
+                for h, count in enumerate(HEADS):
+                    heads_out[h][base + k, e] = code[first : first + count]
+                    first += count
+                sums_out[base + k, 2 * e : 2 * e + 1, :] = jnp.zeros((1, LANES), jnp.float32)
+                sums_out[base + k, 2 * e + 1 : 2 * e + 2, :] = jnp.sum(
+                    jnp.where(beside, most, 0.0), axis=0, keepdims=True
+                )
+
+    def add_sums(i):
         for copy in load(i):
             copy.wait()
         base = plane(i) * ny
         for k in range(ny):
             for g, (e, lo, hi) in enumerate(groups):
-                x = fresh(i, e, k, lo, hi)
-                total = row_sums(x)
-                if lo == 0:
-                    code, most = encode(x[:HEAD])
-                    first = 0
-                    for h, count in enumerate(HEADS):
-                        heads_out[h][base + k, e] = code[first : first + count]
-                        first += count
-                else:
-                    total = total + jnp.sum(jnp.where(beside, most, 0.0), axis=0, keepdims=True)
-                sums_out[base + k, g : g + 1, :] = total
+                sums_out[base + k, g : g + 1, :] += row_sums(fresh(i, e, k, lo, hi))
+
+    before = jnp.where(z < nz // 2 - 1, nz, 0)
+
+    @pl.loop(0, before)
+    def _(i):
+        add_sums(i)
 
     for copy in router:
         copy.wait()
@@ -165,9 +178,17 @@
     pl.semaphore_wait(barrier, n_rows - 1 + n_owner - 1)
 
     for p in far:
+        remote(heads_out[0].at[p], heads_in[0].at[me], head_send.at[0], head_recv.at[0], p).start()
+
+    @pl.loop(before, nz)
+    def _(i):
+        add_sums(i)
+
+    for p in far:
         remote(sums_out.at[p], sums_in.at[me], rs_send, rs_recv, p).start()
-    for p in far:
-        remote(heads_out[0].at[p], heads_in[0].at[me], head_send.at[0], head_recv.at[0], p).start()
+    for h in range(1, len(HEADS) - 1):
+        for p in far:
+            remote(heads_out[h].at[p], heads_in[h].at[me], head_send.at[h], head_recv.at[h], p).start()
 
     sums_in[me] = sums_out[me]
     for h in range(len(HEADS)):
@@ -184,9 +205,9 @@
 
     for p in far:
         remote(mine, scales.at[me], ag_send, ag_recv.at[z], p).start()
-    for h in range(1, len(HEADS)):
-        for p in far:
-            remote(heads_out[h].at[p], heads_in[h].at[me], head_send.at[h], head_recv.at[h], p).start()
+    h = len(HEADS) - 1
+    for p in far:
+        remote(heads_out[h].at[p], heads_in[h].at[me], head_send.at[h], head_recv.at[h], p).start()
     for p in far:
         remote(rpart, rrow.at[me], r1_send, r1_recv, p).start()
 
@@ -322,7 +343,7 @@
             pltpu.VMEM((n_owner, n_rows, 2, lanes), bf16),
             pltpu.VMEM((2 * n_owner, lanes), f32),
             dma, dma, dma,
-            dma((n_rows // ny,)), dma((n_rows // ny,)),
+            dma((2, n_rows // ny)), dma((2, n_rows // ny)),
             dma, dma,
             dma, dma((n_rows // ny,)),
             dma((len(HEADS),)), dma((len(HEADS),)),

time: 90.7 us -> 89.9 us (level); the launches traced: 90.6 us -> 88.4 us
  Pallas kernels: 89.9 us -> 87.8 us
    pallas_call x1, Pallas kernels: 88.1 us -> 85.9 us  [per_device(): pl.pallas_call(functools.partial(exchange, n_rows, n_owner, ny, d_model),...]
where the time goes in v4:
time: 89.9 us; the launch traced here: 88.4 us
  Pallas kernels  87.8 us (98%)
    pallas_call x1, Pallas kernels, per_device(): pl.pallas_call(functools.partial(exchange, n_rows, n_owner, ny, d_model),...  85.9 us
    pallas_call x1, Pallas kernels, per_device(): pl.pallas_call(hand_over, out_shape=tuple((jax.ShapeDtypeStruct(shape, dt...  1.84 us

profile of v4, /device:TPU:1, one launch (start us, length us, event | category | flops | bytes accessed | tf_op | source)
XLA Modules:
  0.0 88.4 jit_solution(5537816388391244031)
XLA Ops:
  0.6 85.9 %shard_map.67 = (bf16[2,200,4096]{2,1,0:T(8,128)(2,1)S(1)}, f32[2,200]{1,0:T(2,128)S(1)}, bf16[16,4096]{1,0:T(8,128)(2,1)S(1)}) custom-call(f32[2,32,200,128]{3,2,1,0:T(8,128)} %bitcast.5, bf16[2,32,200,128]{3,2,1,0:T(8,128)(2,1)} %bitcast.6, f32[2,128]{1,0:T(2,128)} %bitcast.7, f32[1,128]{1,0:T(1,128)} %bitcast.8), custom_call_target="tpu_custom_call" | custom-call | tf_op jit(solution)/shard_map/pallas_call | solution.py:324
  86.6 1.8 %shard_map.68 = (bf16[2,200,4096]{2,1,0:T(8,128)(2,1)}, f32[2,200]{1,0:T(2,128)}, bf16[16,4096]{1,0:T(8,128)(2,1)}) custom-call(bf16[2,200,4096]{2,1,0:T(8,128)(2,1)S(1)} %get-tuple-element.9.serve_ref, f32[2,200]{1,0:T(2,128)S(1)} %get-tuple-element.10.scale_ref, bf16[16,4096]{1,0:T(8,128)(2,1)S(1)} %get-tuple-element.11.router_ref), custom_call_target="tpu_custom_call" | custom-call | tf_op jit(solution)/shard_map/pallas_call | solution.py:358

commit v5 on v4

--- a/solution.py
+++ b/solution.py
@@ -138,8 +138,9 @@
         pieces = jnp.concatenate([one, two, three], axis=1)
         return jnp.dot(pieces, jnp.ones((3 * LANES, LANES), jnp.bfloat16), preferred_element_type=jnp.float32)
 
-    @pl.loop(0, nz)
-    def _(i):
+    before = jnp.where(z < nz // 2 - 1, nz, 0)
+
+    def encode_plane(i):
         for copy in load(i, False):
             copy.wait()
         base = plane(i) * ny
@@ -163,7 +164,9 @@
             for g, (e, lo, hi) in enumerate(groups):
                 sums_out[base + k, g : g + 1, :] += row_sums(fresh(i, e, k, lo, hi))
 
-    before = jnp.where(z < nz // 2 - 1, nz, 0)
+    @pl.loop(0, before)
+    def _(i):
+        encode_plane(i)
 
     @pl.loop(0, before)
     def _(i):
@@ -177,8 +180,18 @@
 
     pl.semaphore_wait(barrier, n_rows - 1 + n_owner - 1)
 
-    for p in far:
-        remote(heads_out[0].at[p], heads_in[0].at[me], head_send.at[0], head_recv.at[0], p).start()
+    @pl.loop(0, nz)
+    def _(i):
+        @pl.when(i >= before)
+        def _():
+            encode_plane(i)
+
+        for k in range(ny):
+            p = plane(i) * ny + lax.rem(y + k, ny)
+
+            @pl.when(p != me)
+            def _():
+                remote(heads_out[0].at[p], heads_in[0].at[me], head_send.at[0], head_recv.at[0], p).start()
 
     @pl.loop(before, nz)
     def _(i):

time: 89.9 us -> 90.7 us (level)
  Pallas kernels: 87.8 us -> 89.5 us
    pallas_call x1, Pallas kernels: 85.9 us -> 87.6 us  [per_device(): pl.pallas_call(functools.partial(exchange, n_rows, n_owner, ny, d_model),...]
where the time goes in v5:
time: 90.7 us; the launch traced here: 90.1 us
  Pallas kernels  89.5 us (99%)
    pallas_call x1, Pallas kernels, per_device(): pl.pallas_call(functools.partial(exchange, n_rows, n_owner, ny, d_model),...  87.6 us
    pallas_call x1, Pallas kernels, per_device(): pl.pallas_call(hand_over, out_shape=tuple((jax.ShapeDtypeStruct(shape, dt...  1.84 us

profile of v5, /device:TPU:1, one launch (start us, length us, event | category | flops | bytes accessed | tf_op | source)
XLA Modules:
  0.0 90.1 jit_solution(9833725242950150405)
XLA Ops:
  0.6 87.6 %shard_map.67 = (bf16[2,200,4096]{2,1,0:T(8,128)(2,1)S(1)}, f32[2,200]{1,0:T(2,128)S(1)}, bf16[16,4096]{1,0:T(8,128)(2,1)S(1)}) custom-call(f32[2,32,200,128]{3,2,1,0:T(8,128)} %bitcast.5, bf16[2,32,200,128]{3,2,1,0:T(8,128)(2,1)} %bitcast.6, f32[2,128]{1,0:T(2,128)} %bitcast.7, f32[1,128]{1,0:T(1,128)} %bitcast.8), custom_call_target="tpu_custom_call" | custom-call | tf_op jit(solution)/shard_map/pallas_call | solution.py:337
  88.3 1.8 %shard_map.68 = (bf16[2,200,4096]{2,1,0:T(8,128)(2,1)}, f32[2,200]{1,0:T(2,128)}, bf16[16,4096]{1,0:T(8,128)(2,1)}) custom-call(bf16[2,200,4096]{2,1,0:T(8,128)(2,1)S(1)} %get-tuple-element.9.serve_ref, f32[2,200]{1,0:T(2,128)S(1)} %get-tuple-element.10.scale_ref, bf16[16,4096]{1,0:T(8,128)(2,1)S(1)} %get-tuple-element.11.router_ref), custom_call_target="tpu_custom_call" | custom-call | tf_op jit(solution)/shard_map/pallas_call | solution.py:371
